TPU v7x, 512 devices: a whole 4x8x8 slice. The times are simulated.
512 devices in a mesh: seq: 8 (over z), mp: 16 (over y, core), dp: 4 (over x).
Axes of the slice: x: 4, y: 8, z: 8, core: 2. Of those that a mesh axis runs over, the one named last changes fastest.
Arguments:
- tokens: bfloat16 [65536, 2048], P(('dp', 'seq'), 'mp'), parts along dimension 0, may hold values from -6 to 6
- w_query: bfloat16 [2048, 2048], P(None, 'mp'), may hold values from -0.125 to 0.125
- w_key: bfloat16 [2048, 2048], P(None, 'mp'), may hold values from -0.125 to 0.125
- w_value: bfloat16 [2048, 2048], P(None, 'mp'), may hold values from -0.125 to 0.125
- w_gate: bfloat16 [2048, 2048], P(None, 'mp'), may hold values from -0.125 to 0.125
- decay_exponent: int32 [16], P('mp'), may hold values from 5 to 16
- forget: float32 [65536, 16], P(('dp', 'seq'), 'mp'), parts along dimension 0, may hold values from 0 to 0.69
- norm_gain: float32 [2048], replicated, may hold values from 0.1 to 1.9
Outputs:
- retained: bfloat16 [65536, 2048], P(('dp', 'seq', 'mp')), parts along dimension 0
There are 4 independent parts, one for each index of `dp`. A program takes and returns all parts, laid end to end along the dimension named above; an argument that names none is the same for every part. Nothing has to cross between parts.
All inputs are finite; a program needn't handle non-finite values.
Results may differ from a plain program's by a relative error of at most 0.015.
Values may be sent and summed in bfloat16 or wider, within the bound.
A program may use at most 64 MiB of HBM per device.

v0:
```python
import jax
import jax.numpy as jnp
from jax import lax
from jax.sharding import PartitionSpec as P

HEADS = 16
DH = 128


def from_everyone(shard, axis):
    copies = jnp.broadcast_to(shard, (lax.axis_size(axis), *shard.shape))
    return lax.all_to_all(copies, axis, split_axis=0, concat_axis=0, tiled=True)


def collected_together(shard, axis):
    leaves = jax.tree.leaves(shard)
    sequence = sorted(range(len(leaves)), key=lambda k: -leaves[k].size)
    width = (1, *leaves[sequence[0]].shape)[-1]
    lines = [
        jnp.pad(leaves[k].reshape(-1), (0, -leaves[k].size % width)).reshape(-1, width)
        for k in sequence
    ]
    both, at, found = (from_everyone(jnp.concatenate(lines), axis), 0, {})
    for k, line in zip(sequence, lines):
        section = both[:, at : at + len(line)].reshape(len(both), -1)
        found[k] = section[:, : leaves[k].size].reshape(-1, *leaves[k].shape)
        at += len(line)
    numbers = iter(range(len(leaves)))
    return jax.tree.map(lambda _: found[next(numbers)], shard)


def folded_in_pairs(pieces, combine):
    while len(jax.tree.leaves(pieces)[0]) > 1:
        pieces = jax.vmap(combine)(
            *(jax.tree.map(lambda part: part[side::2], pieces) for side in (0, 1))
        )
    return jax.tree.map(lambda part: part[0], pieces)


def prefix_2(shard, axis, combine, identity):
    size, index = (lax.axis_size(axis), lax.axis_index(axis))
    passed = jnp.arange(size) < index

    def kept(part, zero, own):
        part = jnp.where(
            passed.reshape(-1, *(1 for _ in own.shape)),
            part.astype(own.dtype),
            jnp.asarray(zero, own.dtype),
        )
        return part

    pieces = collected_together(
        jax.tree.map(lambda part, kind: part.astype(kind), shard, (jnp.bfloat16, jnp.bfloat16)),
        axis,
    )
    return folded_in_pairs(jax.tree.map(kept, pieces, identity, shard), combine)


def over_copies(shard, axis):
    return from_everyone(shard, axis).sum(axis=0)


def run_blocks(queries, key_rows, values, logdecay, head_count, head_width):
    seq_rows = queries.shape[0]
    block_rows = 512
    block_count = seq_rows // block_rows

    def shaped(source):
        return source.reshape(block_count, block_rows, head_count, head_width)

    decays = logdecay.reshape(block_count, block_rows, head_count)
    position = lax.broadcasted_iota(jnp.int32, (block_rows, block_rows), 0)
    earlier = lax.broadcasted_iota(jnp.int32, (block_rows, block_rows), 1)
    causal = position >= earlier

    def advance(carried, pieces):
        kv_state, offset = carried
        query_blk, key_blk, value_blk, decay_blk = pieces
        running = jnp.cumsum(decay_blk, axis=0)
        heads_first = running.T
        log_gap = heads_first[:, :, None] - heads_first[:, None, :]
        decay_mask = jnp.where(causal[None], jnp.exp(jnp.where(causal[None], log_gap, 0.0)), 0.0)
        scores = jnp.einsum("tha,sha->hts", query_blk, key_blk, preferred_element_type=jnp.float32)
        scores = (scores * decay_mask).astype(jnp.bfloat16)
        inner = jnp.einsum("hts,shb->thb", scores, value_blk, preferred_element_type=jnp.float32)
        query_float = query_blk.astype(jnp.float32)
        earlier_part = jnp.einsum(
            "tha,hab->thb", query_float * jnp.exp(running)[:, :, None], kv_state
        )
        query_device = query_float * jnp.exp(running + offset[None, :])[:, :, None]
        key_scaled = key_blk.astype(jnp.float32) * jnp.exp(running[-1:] - running)[:, :, None]
        kv_state = jnp.exp(running[-1])[:, None, None] * kv_state + jnp.einsum(
            "sha,shb->hab", key_scaled, value_blk.astype(jnp.float32)
        )
        return ((kv_state, offset + running[-1]), (inner + earlier_part, query_device))

    initial = (
        jnp.zeros((head_count, head_width, head_width), jnp.float32),
        jnp.zeros((head_count,), jnp.float32),
    )
    final, outputs = lax.scan(
        advance, initial, (shaped(queries), shaped(key_rows), shaped(values), decays)
    )
    local_part = outputs[0].reshape(seq_rows, head_count, head_width)
    query_device = outputs[1].reshape(seq_rows, head_count, head_width)
    return (local_part, query_device, final[0], final[1])


def combine_states(before, after):
    return (before[0] * after[0], after[0][:, None, None] * before[1] + after[1])


def body(tokens, w_query, w_key, w_value, w_gate, decay_exponent, forget, norm_gain):
    seq_rows = tokens.shape[0]
    local_width = w_query.shape[1]
    head_count = decay_exponent.shape[0]
    head_width = local_width // head_count
    empty = jnp.zeros((seq_rows, local_width), jnp.float32)
    summed = (empty, empty, empty, empty)
    piece = lax.all_gather(tokens, "mp", axis=1, tiled=True)
    results = []
    for weight, partial_value in zip((w_query, w_key, w_value, w_gate), summed):
        results.append(jnp.dot(piece, weight, preferred_element_type=jnp.float32))
    projected = tuple(results)
    queries = projected[0].astype(jnp.bfloat16)
    key_rows = (projected[1] * DH ** (-0.5)).astype(jnp.bfloat16)
    values = projected[2].astype(jnp.bfloat16)
    gate = projected[3].astype(jnp.bfloat16)
    rate = jnp.log1p(-jnp.exp2(-decay_exponent.astype(jnp.float32)))
    logdecay = rate[None, :] - forget
    local_part, query_device, own_state, own_total = run_blocks(
        queries, key_rows, values, logdecay, head_count, head_width
    )
    prefix = prefix_2(
        (jnp.exp(own_total), own_state),
        "seq",
        combine_states,
        (jnp.ones_like(own_total), jnp.zeros_like(own_state)),
    )
    incoming = prefix[1]
    from_before = jnp.einsum("tha,hab->thb", query_device, incoming)
    output = (local_part + from_before).astype(jnp.bfloat16).reshape(seq_rows, local_width)
    output_float = output.astype(jnp.float32)
    squares = over_copies(jnp.sum(output_float * output_float, axis=1), "mp")
    rstd = lax.rsqrt(squares / (HEADS * DH) + 1e-06)
    gain_here = lax.dynamic_slice_in_dim(
        norm_gain, lax.axis_index("mp") * local_width, local_width, 0
    )
    gated = (
        jax.nn.silu(gate.astype(jnp.float32)) * output_float * rstd[:, None] * gain_here[None, :]
    )
    return lax.all_to_all(gated.astype(jnp.bfloat16), "mp", split_axis=0, concat_axis=1, tiled=True)


def solution(mesh):
    placed = (
        P(("dp", "seq"), "mp"),
        P(None, "mp"),
        P(None, "mp"),
        P(None, "mp"),
        P(None, "mp"),
        P("mp"),
        P(("dp", "seq"), "mp"),
        P(),
    )
    return jax.shard_map(
        body, mesh=mesh, in_specs=placed, out_specs=P(("dp", "seq", "mp"), None), check_vma=False
    )
```

profile of v0, /device:TPU:1, one launch (start us, length us, event | category | flops | bytes accessed | tf_op | source)
XLA Modules:
  0.0 194.3 jit_solution(12837014939397995423)
XLA Ops:
  8.7 76.1 %all-gather.2.cloned.1.call-done = bf16[2048,2048]{1,0:T(8,128)(2,1)} async-done(((bf16[2048,128]{1,0:T(8,128)(2,1)}), bf16[2048,2048]{1,0:T(8,128)(2,1)}) %all-gather.2.cloned.1.call-update) | async-done | bytes 8388624 | tf_op jit(solution)/shard_map/all_gather | solution.py:120
  84.8 5.9 %fusion.52 = bf16[2048,128]{1,0:T(8,128)(2,1)S(1)} fusion(bf16[2048,2048]{1,0:T(8,128)(2,1)} %all-gather.2.cloned.1.call-done, bf16[2048,128]{1,0:T(8,128)(2,1)S(1)} %copy-done), kind=kOutput, calls=%fused_computation.61 | convolution fusion | flops 1074266112 | bytes 9437184 | tf_op jit(solution)/shard_map/dot_general | solution.py:123
  90.7 3.3 %convolution_convert_fusion.1 = bf16[2048,128]{1,0:T(8,128)(2,1)} fusion(bf16[2048,2048]{1,0:T(8,128)(2,1)S(1)} %copy-done.1, bf16[2048,128]{1,0:T(8,128)(2,1)S(1)} %copy-done.2), kind=kOutput, calls=%fused_computation.57 | convolution fusion | flops 1074003968 | bytes 9437184 | tf_op jit(solution)/shard_map/dot_general | solution.py:123
  94.0 2.4 %convolution_convert_fusion = bf16[2048,128]{1,0:T(8,128)(2,1)S(1)} fusion(bf16[2048,2048]{1,0:T(8,128)(2,1)S(1)} %copy-done.1, bf16[2048,128]{1,0:T(8,128)(2,1)S(1)} %copy-done.3), kind=kOutput, calls=%fused_computation.56 | convolution fusion | flops 1074003968 | bytes 9437184 | tf_op jit(solution)/shard_map/dot_general | solution.py:123
  96.4 29.3 %while.18 = (s32[]{:T(128)}, f32[1,128,128]{2,1,0:T(8,128)S(1)}, f32[1]{0:T(128)}, f32[4,512,1,128]{3,1,0,2:T(8,128)S(1)}, bf16[4,512,1,128]{3,1,2,0:T(8,128)(2,...) while((s32[]{:T(128)}, f32[1,128,128]{2,1,0:T(8,128)S(1)}, ...), condition=%wide.region_3.4_spmd.clone.clone, body=%wide.region_0.3_spmd.clone.clone.sunk | while | flops 169935888 | bytes 3247952 | solution.py:101
  99.9 1.5 fusion.91
  101.6 1.3 fusion.90
  102.9 0.8 fusion.92
  107.3 1.5 fusion.91
  108.9 1.3 fusion.90
  110.2 0.8 fusion.92
  114.6 1.5 fusion.91
  116.2 1.3 fusion.90
  117.5 0.8 fusion.92
  121.9 1.5 fusion.91
  123.5 1.3 fusion.90
  126.5 4.0 %all-to-all-start = ((bf16[8,129,128]{2,1,0:T(8,128)(2,1)}), bf16[8,129,128]{2,1,0:T(8,128)(2,1)S(1)}, u32[]{:S(2)}, u32[]{:S(2)}) async-start(bf16[8,129,128]{2,1,0:T(8,128)(2,1)} %broadcast_in_dim.45), calls=%async_computation | async-start | bytes 557056 | tf_op jit(solution)/shard_map/all_to_all | solution.py:12
  130.5 12.5 %all-to-all-done = bf16[8,129,128]{2,1,0:T(8,128)(2,1)S(1)} async-done(((bf16[8,129,128]{2,1,0:T(8,128)(2,1)}), bf16[8,129,128]{2,1,0:T(8,128)(2,1)S(1)}, u32[]{:S(2)}, u32[]{:S(2)}) %all-to-all-start) | async-done | bytes 264224 | tf_op jit(solution)/shard_map/all_to_all | solution.py:12
  144.2 2.1 %multiply_reduce_fusion = (f32[2048]{0:T(1024)S(1)}, f32[2048,128]{1,0:T(8,128)S(1)}) fusion(f32[2048,1,128]{2,0,1:T(8,128)S(1)} %bitcast.167, bf16[2048,128]{1,0:T(8,128)(2,1)} %bitcast.171, f32[2,1,128,128]{3,2,1,0:T(8,128)S(1)} %slice_add_fusion.1, f32[]{:T(128)} %bitcast.12), kind=kOutput, calls=%fused_computation.65 | convolution fusion | flops 68450304 | bytes 2760708 | tf_op jit(solution)/shard_map/tha,hab->thb/dot_general | solution.py:141
  147.0 4.9 %all-to-all-start.1 = ((f32[16,1,2048]{2,1,0:T(1,128)}), f32[16,1,2048]{2,1,0:T(1,128)S(1)}, u32[]{:S(2)}, u32[]{:S(2)}) async-start(f32[16,1,2048]{2,1,0:T(1,128)} %broadcast_in_dim.49), calls=%async_computation.1 | async-start | bytes 262144 | tf_op jit(solution)/shard_map/all_to_all | solution.py:12
  152.7 8.1 %all-to-all-done.1 = f32[16,1,2048]{2,1,0:T(1,128)S(1)} async-done(((f32[16,1,2048]{2,1,0:T(1,128)}), f32[16,1,2048]{2,1,0:T(1,128)S(1)}, u32[]{:S(2)}, u32[]{:S(2)}) %all-to-all-start.1) | async-done | bytes 131104 | tf_op jit(solution)/shard_map/all_to_all | solution.py:12
  160.9 5.8 %multiply_convert_fusion = bf16[2048,128]{1,0:T(8,128)(2,1)S(1)} fusion(f32[2048,128]{1,0:T(8,128)S(1)} %get-tuple-element.204, bf16[2048,2048]{1,0:T(8,128)(2,1)} %all-gather.2.cloned.1.call-done, bf16[2048,128]{1,0:T(8,128)(2,1)} %param.14, f32[128]{0:T(128)S(1)} %dynamic_slice.17, f32[2048]{0:T(1024)S(1)} %add_rsqrt_fusion), kind=kOutput, calls=%fused_computation.64 | convolution fusion | flops 1076363264 | bytes 10494464 | tf_op jit(solution)/shard_map/dot_general | solution.py:123
  166.7 19.9 %all_to_all.30 = bf16[16,128,128]{2,1,0:T(8,128)(2,1)S(1)} all-to-all(bf16[16,128,128]{2,1,0:T(8,128)(2,1)S(1)} %bitcast.170), channel_id=1, replica_groups=mesh['seq'=8,'mp'=16,'dp'=4] {'mp'}, dimensions={0} | all-to-all | bytes 1048576 | tf_op jit(solution)/shard_map/all_to_all | solution.py:152
  186.6 0.9 copy_bitcast_fusion
  (89 shorter events, 15.7 us)
Async XLA Ops:
  6.5 78.2 %copy-start = (bf16[2048,128]{1,0:T(8,128)(2,1)S(1)}, bf16[2048,128]{1,0:T(8,128)(2,1)}, u32[]{:S(2)}) copy-start(bf16[2048,128]{1,0:T(8,128)(2,1)} %param.12) | copy-start | bytes 1572868
  6.5 84.1 %copy-start.2 = (bf16[2048,128]{1,0:T(8,128)(2,1)S(1)}, bf16[2048,128]{1,0:T(8,128)(2,1)}, u32[]{:S(2)}) copy-start(bf16[2048,128]{1,0:T(8,128)(2,1)} %param.13) | copy-start | bytes 1572868
  6.5 78.2 %all-gather.2.cloned.1.call-start = ((), (), s32[]{:S(2)}) async-start(), calls=%async_computation.3 | async-start | bytes 8912896 | tf_op jit(solution)/shard_map/all_gather | solution.py:120
  84.8 5.9 %copy-start.1 = (bf16[2048,2048]{1,0:T(8,128)(2,1)S(1)}, bf16[2048,2048]{1,0:T(8,128)(2,1)}, u32[]{:S(2)}) copy-start(bf16[2048,2048]{1,0:T(8,128)(2,1)} %all-gather.2.cloned.1.call-done) | copy-start | bytes 25165828
  90.7 3.3 %copy-start.3 = (bf16[2048,128]{1,0:T(8,128)(2,1)S(1)}, bf16[2048,128]{1,0:T(8,128)(2,1)}, u32[]{:S(2)}) copy-start(bf16[2048,128]{1,0:T(8,128)(2,1)} %param.11) | copy-start | bytes 1572868
  126.5 16.6 %all-to-all-start = ((bf16[8,129,128]{2,1,0:T(8,128)(2,1)}), bf16[8,129,128]{2,1,0:T(8,128)(2,1)S(1)}, u32[]{:S(2)}, u32[]{:S(2)}) async-start(bf16[8,129,128]{2,1,0:T(8,128)(2,1)} %broadcast_in_dim.45), calls=%async_computation | async-start | bytes 557056 | tf_op jit(solution)/shard_map/all_to_all | solution.py:12
  147.0 13.8 %all-to-all-start.1 = ((f32[16,1,2048]{2,1,0:T(1,128)}), f32[16,1,2048]{2,1,0:T(1,128)S(1)}, u32[]{:S(2)}, u32[]{:S(2)}) async-start(f32[16,1,2048]{2,1,0:T(1,128)} %broadcast_in_dim.49), calls=%async_computation.1 | async-start | bytes 262144 | tf_op jit(solution)/shard_map/all_to_all | solution.py:12
Sparse Core Ops, SparseCore 0:
  9.4 75.3 all-gather.1
where the time goes:
time: 195 us; the launch traced here: 194 us
  waiting for transfers between devices  97.4 us (50%)
  matrix products  31.5 us (16%)
  blocking collectives  19.9 us (10%)
  between operations  14.3 us (7%)
  local copies, waits for them, and re-layouts  10.2 us (5%)
  starting transfers between devices  8.92 us (5%)
  other arithmetic  6.83 us (4%)
  loops' own time  5.24 us (3%)
    all_gather x1, waiting for transfers between devices, body(): piece = lax.all_gather(tokens, 'mp', axis=1, tiled=True)  76.1 us
    all_to_all x2, waiting for transfers between devices, from_everyone(): return lax.all_to_all(copies, axis, split_axis=0, concat_axis=0, tiled=True)  20.7 us
    all_to_all x1, blocking collectives, body(): lax.all_to_all(gated.astype(jnp.bfloat16), 'mp', split_axis=0, concat_axi...  19.9 us
    dot_general x4, matrix products, body(): results.append(jnp.dot(piece, weight, preferred_element_type=jnp.float32))  17.3 us
    all_to_all x2, starting transfers between devices, from_everyone(): return lax.all_to_all(copies, axis, split_axis=0, concat_axis=0, tiled=True)  8.92 us
    dot_general x4, matrix products, advance(): jnp.einsum('hts,shb->thb', scores, value_blk, preferred_element_type=jnp....  5.87 us
    another operation x1, loops' own time, run_blocks(): lax.scan(advance, initial, (shaped(queries), shaped(key_rows), shaped(val...  5.24 us
    dot_general x4, matrix products, advance(): jnp.einsum('sha,shb->hab', key_scaled, value_blk.astype(jnp.float32))  5.01 us
  transfers between devices with their start and end apart: 3, of which 3 were waited for; matrix products, arithmetic and copies ran while one was open for 1% of the time, Pallas kernels for 0%

commit v1 on v0

--- a/solution.py
+++ b/solution.py
@@ -117,7 +117,21 @@
     head_width = local_width // head_count
     empty = jnp.zeros((seq_rows, local_width), jnp.float32)
     summed = (empty, empty, empty, empty)
-    piece = lax.all_gather(tokens, "mp", axis=1, tiled=True)
+    ways, here, turn = (lax.axis_size("mp"), lax.axis_index("mp"), tokens.shape[1])
+    shape = [n * ways if d == 1 else n for d, n in enumerate(tokens.shape)]
+    full = lax.dynamic_update_slice_in_dim(
+        jnp.zeros(shape, tokens.dtype), tokens, here * turn, axis=1
+    )
+    going_up = going_down = tokens
+    for far in range(1, ways // 2 + 1):
+        going_up = lax.ppermute(going_up, "mp", [(d, (d + 1) % ways) for d in range(ways)])
+        full = lax.dynamic_update_slice_in_dim(full, going_up, (here - far) % ways * turn, axis=1)
+        if 2 * far < ways:
+            going_down = lax.ppermute(going_down, "mp", [(d, (d - 1) % ways) for d in range(ways)])
+            full = lax.dynamic_update_slice_in_dim(
+                full, going_down, (here + far) % ways * turn, axis=1
+            )
+    piece = full
     results = []
     for weight, partial_value in zip((w_query, w_key, w_value, w_gate), summed):
         results.append(jnp.dot(piece, weight, preferred_element_type=jnp.float32))

time: 195 us -> 201 us (1.031)
  waiting for transfers between devices: 97.4 us -> 26.5 us
  starting transfers between devices: 8.92 us -> 68.9 us
  local copies, waits for them, and re-layouts: 10.2 us -> 33.5 us
  between operations: 14.3 us -> 0.93 us
  matrix products: 31.5 us -> 38.1 us
    all_gather x1 -> x0, waiting for transfers between devices: 76.1 us -> none  [body(): piece = lax.all_gather(tokens, 'mp', axis=1, tiled=True)]
    ppermute x0 -> x15, starting transfers between devices: none -> 47.8 us  [the longest x7 39.3 us: body(): lax.ppermute(going_down, 'mp', [(d, (d - 1) % ways) for d in range(ways)])]
    dynamic_update_slice x0 -> x16, local copies, waits for them, and re-layouts: none -> 18.6 us  [the longest x8 9.22 us: body(): lax.dynamic_update_slice_in_dim(full, going_up, (here - far) % ways * tur...]
    all_to_all x2, starting transfers between devices: 8.92 us -> 21 us  [from_everyone(): return lax.all_to_all(copies, axis, split_axis=0, concat_axis=0, tiled=True)]
    ppermute x0 -> x15, waiting for transfers between devices: none -> 8.9 us  [the longest x8 7.23 us: body(): lax.ppermute(going_up, 'mp', [(d, (d + 1) % ways) for d in range(ways)])]
    dot_general x4, matrix products: 17.3 us -> 23.9 us  [body(): results.append(jnp.dot(piece, weight, preferred_element_type=jnp.float32))]
    broadcast_in_dim x0 -> x1, local copies, waits for them, and re-layouts: none -> 4.29 us  [body(): jnp.zeros(shape, tokens.dtype)]
    all_to_all x2, waiting for transfers between devices: 20.7 us -> 17.6 us  [from_everyone(): return lax.all_to_all(copies, axis, split_axis=0, concat_axis=0, tiled=True)]
  transfers between devices with their start and end apart: 3 -> 17, of which waited for: 3 -> 7; matrix products, arithmetic and copies ran while one was open for 1% -> 12% of each run, Pallas kernels for 0% -> 0%
where the time goes in v1:
time: 201 us; the launch traced here: 200 us
  starting transfers between devices  68.9 us (34%)
  matrix products  38.1 us (19%)
  local copies, waits for them, and re-layouts  33.5 us (17%)
  waiting for transfers between devices  26.5 us (13%)
  blocking collectives  19.9 us (10%)
  other arithmetic  6.83 us (3%)
  loops' own time  5.66 us (3%)
    ppermute x7, starting transfers between devices, body(): lax.ppermute(going_down, 'mp', [(d, (d - 1) % ways) for d in range(ways)])  39.3 us
    dot_general x4, matrix products, body(): results.append(jnp.dot(piece, weight, preferred_element_type=jnp.float32))  23.9 us
    all_to_all x2, starting transfers between devices, from_everyone(): return lax.all_to_all(copies, axis, split_axis=0, concat_axis=0, tiled=True)  21 us
    all_to_all x1, blocking collectives, body(): lax.all_to_all(gated.astype(jnp.bfloat16), 'mp', split_axis=0, concat_axi...  19.9 us
    all_to_all x2, waiting for transfers between devices, from_everyone(): return lax.all_to_all(copies, axis, split_axis=0, concat_axis=0, tiled=True)  17.6 us
    dynamic_update_slice x8, local copies, waits for them, and re-layouts, body(): lax.dynamic_update_slice_in_dim(full, going_up, (here - far) % ways * tur...  9.22 us
    ppermute x8, starting transfers between devices, body(): lax.ppermute(going_up, 'mp', [(d, (d + 1) % ways) for d in range(ways)])  8.48 us
    dynamic_update_slice x7, local copies, waits for them, and re-layouts, body(): lax.dynamic_update_slice_in_dim(full, going_down, (here + far) % ways * t...  8.43 us
  transfers between devices with their start and end apart: 17, of which 7 were waited for; matrix products, arithmetic and copies ran while one was open for 12% of the time, Pallas kernels for 0%

profile of v1, /device:TPU:1, one launch (start us, length us, event | category | flops | bytes accessed | tf_op | source)
XLA Modules:
  0.0 200.3 jit_solution(5323872683217348478)
XLA Ops:
  0.0 2.7 %collective-permute-start = (bf16[2048,128]{1,0:T(8,128)(2,1)}, bf16[2048,128]{1,0:T(8,128)(2,1)S(1)}, u32[]{:S(2)}, u32[]{:S(2)}) collective-permute-start(bf16[2048,128]{1,0:T(8,128)(2,1)} %param.10), channel_id=1, source_target_pairs={{0,4},{4,8},{8,12},{12,16},{16,20},{20,24},{24,28},{28,32},{32,36}... | collective-permute-start | bytes 1572872 | tf_op jit(solution)/shard_map/ppermute | solution.py:127
  2.7 4.2 %collective-permute-start.1 = (bf16[2048,128]{1,0:T(8,128)(2,1)}, bf16[2048,128]{1,0:T(8,128)(2,1)S(1)}, u32[]{:S(2)}, u32[]{:S(2)}) collective-permute-start(bf16[2048,128]{1,0:T(8,128)(2,1)} %param.10), channel_id=1, source_target_pairs={{0,60},{4,0},{8,4},{12,8},{16,12},{20,16},{24,20},{28,24},{32,28},... | collective-permute-start | bytes 1572872 | tf_op jit(solution)/shard_map/ppermute | solution.py:130
  6.8 2.8 %collective-permute-done = bf16[2048,128]{1,0:T(8,128)(2,1)S(1)} collective-permute-done((bf16[2048,128]{1,0:T(8,128)(2,1)}, bf16[2048,128]{1,0:T(8,128)(2,1)S(1)}, u32[]{:S(2)}, u32[]{:S(2)}) %collective-permute-start) | collective-permute-done | bytes 524320 | tf_op jit(solution)/shard_map/ppermute | solution.py:127
  9.7 2.4 %collective-permute-start.2 = (bf16[2048,128]{1,0:T(8,128)(2,1)S(1)}, bf16[2048,128]{1,0:T(8,128)(2,1)S(1)}, u32[]{:S(2)}, u32[]{:S(2)}) collective-permute-start(bf16[2048,128]{1,0:T(8,128)(2,1)S(1)} %collective-permute-done), channel_id=1, source_target_pairs={{0,4},{4,8},{8,12},{12,16},{16,20},{20,24},{24,28},{28,32},{32,36}... | collective-permute-start | bytes 1572872 | tf_op jit(solution)/shard_map/ppermute | solution.py:127
  12.0 4.9 %collective-permute-start.3 = (bf16[2048,128]{1,0:T(8,128)(2,1)S(1)}, bf16[2048,128]{1,0:T(8,128)(2,1)S(1)}, u32[]{:S(2)}, u32[]{:S(2)}) collective-permute-start(bf16[2048,128]{1,0:T(8,128)(2,1)S(1)} %collective-permute-done.1), channel_id=1, source_target_pairs={{0,60},{4,0},{8,4},{12,8},{16,12},{20,16},{24,20},{28,24},{32,28},... | collective-permute-start | bytes 1572872 | tf_op jit(solution)/shard_map/ppermute | solution.py:130
  18.3 2.4 %collective-permute-start.4 = (bf16[2048,128]{1,0:T(8,128)(2,1)S(1)}, bf16[2048,128]{1,0:T(8,128)(2,1)S(1)}, u32[]{:S(2)}, u32[]{:S(2)}) collective-permute-start(bf16[2048,128]{1,0:T(8,128)(2,1)S(1)} %collective-permute-done.2), channel_id=1, source_target_pairs={{0,4},{4,8},{8,12},{12,16},{16,20},{20,24},{24,28},{28,32},{32,36}... | collective-permute-start | bytes 1572872 | tf_op jit(solution)/shard_map/ppermute | solution.py:127
  21.4 6.1 %collective-permute-start.5 = (bf16[2048,128]{1,0:T(8,128)(2,1)S(1)}, bf16[2048,128]{1,0:T(8,128)(2,1)}, u32[]{:S(2)}, u32[]{:S(2)}) collective-permute-start(bf16[2048,128]{1,0:T(8,128)(2,1)S(1)} %collective-permute-done.3), channel_id=1, source_target_pairs={{0,60},{4,0},{8,4},{12,8},{16,12},{20,16},{24,20},{28,24},{32,28},... | collective-permute-start | bytes 1572872 | tf_op jit(solution)/shard_map/ppermute | solution.py:130
  29.2 4.3 %broadcast_in_dim.48 = bf16[2048,2048]{1,0:T(8,128)(2,1)} broadcast(bf16[]{:T(256)} %constant.127.clone.1), dimensions={} | broadcast | bytes 8388610 | tf_op jit(solution)/shard_map/broadcast_in_dim | solution.py:123
  36.4 7.3 %collective-permute-start.7 = (bf16[2048,128]{1,0:T(8,128)(2,1)}, bf16[2048,128]{1,0:T(8,128)(2,1)S(1)}, u32[]{:S(2)}, u32[]{:S(2)}) collective-permute-start(bf16[2048,128]{1,0:T(8,128)(2,1)} %collective-permute-done.5), channel_id=1, source_target_pairs={{0,60},{4,0},{8,4},{12,8},{16,12},{20,16},{24,20},{28,24},{32,28},... | collective-permute-start | bytes 1572872 | tf_op jit(solution)/shard_map/ppermute | solution.py:130
  47.4 6.2 %collective-permute-start.9 = (bf16[2048,128]{1,0:T(8,128)(2,1)S(1)}, bf16[2048,128]{1,0:T(8,128)(2,1)S(1)}, u32[]{:S(2)}, u32[]{:S(2)}) collective-permute-start(bf16[2048,128]{1,0:T(8,128)(2,1)S(1)} %collective-permute-done.7), channel_id=1, source_target_pairs={{0,60},{4,0},{8,4},{12,8},{16,12},{20,16},{24,20},{28,24},{32,28},... | collective-permute-start | bytes 1572872 | tf_op jit(solution)/shard_map/ppermute | solution.py:130
  58.4 4.9 %collective-permute-start.11 = (bf16[2048,128]{1,0:T(8,128)(2,1)S(1)}, bf16[2048,128]{1,0:T(8,128)(2,1)S(1)}, u32[]{:S(2)}, u32[]{:S(2)}) collective-permute-start(bf16[2048,128]{1,0:T(8,128)(2,1)S(1)} %collective-permute-done.9), channel_id=1, source_target_pairs={{0,60},{4,0},{8,4},{12,8},{16,12},{20,16},{24,20},{28,24},{32,28},... | collective-permute-start | bytes 1572872 | tf_op jit(solution)/shard_map/ppermute | solution.py:130
  67.3 5.8 %collective-permute-start.13 = (bf16[2048,128]{1,0:T(8,128)(2,1)S(1)}, bf16[2048,128]{1,0:T(8,128)(2,1)S(1)}, u32[]{:S(2)}, u32[]{:S(2)}) collective-permute-start(bf16[2048,128]{1,0:T(8,128)(2,1)S(1)} %collective-permute-done.11), channel_id=1, source_target_pairs={{0,60},{4,0},{8,4},{12,8},{16,12},{20,16},{24,20},{28,24},{32,28},... | collective-permute-start | bytes 1572872 | tf_op jit(solution)/shard_map/ppermute | solution.py:130
  77.1 3.0 %collective-permute-done.14 = bf16[2048,128]{1,0:T(8,128)(2,1)S(1)} collective-permute-done((bf16[2048,128]{1,0:T(8,128)(2,1)S(1)}, bf16[2048,128]{1,0:T(8,128)(2,1)S(1)}, u32[]{:S(2)}, u32[]{:S(2)}) %collective-permute-start.14) | collective-permute-done | bytes 524320 | tf_op jit(solution)/shard_map/ppermute | solution.py:127
  81.1 5.7 %fusion.52 = bf16[2048,128]{1,0:T(8,128)(2,1)S(1)} fusion(bf16[2048,2048]{1,0:T(8,128)(2,1)} %constant_dynamic-update-slice_fusion.1, bf16[2048,128]{1,0:T(8,128)(2,1)S(1)} %copy-done), kind=kOutput, calls=%fused_computation.61 | convolution fusion | flops 1074266112 | bytes 9437184 | tf_op jit(solution)/shard_map/dot_general | solution.py:137
  86.8 6.6 %convolution_convert_fusion.1 = bf16[2048,128]{1,0:T(8,128)(2,1)} fusion(bf16[2048,2048]{1,0:T(8,128)(2,1)} %constant_dynamic-update-slice_fusion.1, bf16[2048,128]{1,0:T(8,128)(2,1)S(1)} %copy-done.4), kind=kOutput, calls=%fused_computation.57 | convolution fusion | flops 1074003968 | bytes 9437184 | tf_op jit(solution)/shard_map/dot_general | solution.py:137
  93.5 5.7 %convolution_convert_fusion = bf16[2048,128]{1,0:T(8,128)(2,1)S(1)} fusion(bf16[2048,2048]{1,0:T(8,128)(2,1)} %constant_dynamic-update-slice_fusion.1, bf16[2048,128]{1,0:T(8,128)(2,1)S(1)} %copy-done.5), kind=kOutput, calls=%fused_computation.56 | convolution fusion | flops 1074003968 | bytes 9437184 | tf_op jit(solution)/shard_map/dot_general | solution.py:137
  99.2 30.1 %while.18 = (s32[]{:T(128)}, f32[1,128,128]{2,1,0:T(8,128)S(1)}, f32[1]{0:T(128)}, f32[4,512,1,128]{3,1,0,2:T(8,128)S(1)}, bf16[4,512,1,128]{3,1,2,0:T(8,128)(2,...) while((s32[]{:T(128)}, f32[1,128,128]{2,1,0:T(8,128)S(1)}, ...), condition=%wide.region_3.4_spmd.clone.clone, body=%wide.region_0.3_spmd.clone.clone.sunk | while | flops 169935888 | bytes 3247952 | solution.py:101
  130.1 4.7 %all-to-all-start = ((bf16[8,129,128]{2,1,0:T(8,128)(2,1)}), bf16[8,129,128]{2,1,0:T(8,128)(2,1)S(1)}, u32[]{:S(2)}, u32[]{:S(2)}) async-start(bf16[8,129,128]{2,1,0:T(8,128)(2,1)} %broadcast_in_dim.49), calls=%async_computation | async-start | bytes 557056 | tf_op jit(solution)/shard_map/all_to_all | solution.py:12
  134.8 9.5 %all-to-all-done = bf16[8,129,128]{2,1,0:T(8,128)(2,1)S(1)} async-done(((bf16[8,129,128]{2,1,0:T(8,128)(2,1)}), bf16[8,129,128]{2,1,0:T(8,128)(2,1)S(1)}, u32[]{:S(2)}, u32[]{:S(2)}) %all-to-all-start) | async-done | bytes 264224 | tf_op jit(solution)/shard_map/all_to_all | solution.py:12
  145.6 2.2 %multiply_reduce_fusion = (f32[2048]{0:T(1024)S(1)}, f32[2048,128]{1,0:T(8,128)S(1)}) fusion(f32[2048,1,128]{2,0,1:T(8,128)S(1)} %bitcast.167, bf16[2048,128]{1,0:T(8,128)(2,1)} %bitcast.171, f32[2,1,128,128]{3,2,1,0:T(8,128)S(1)} %slice_add_fusion.1, f32[]{:T(128)} %bitcast.12), kind=kOutput, calls=%fused_computation.65 | convolution fusion | flops 68450304 | bytes 2760708 | tf_op jit(solution)/shard_map/tha,hab->thb/dot_general | solution.py:155
  148.5 16.3 %all-to-all-start.1 = ((f32[16,1,2048]{2,1,0:T(1,128)}), f32[16,1,2048]{2,1,0:T(1,128)S(1)}, u32[]{:S(2)}, u32[]{:S(2)}) async-start(f32[16,1,2048]{2,1,0:T(1,128)} %broadcast_in_dim.53), calls=%async_computation.1 | async-start | bytes 262144 | tf_op jit(solution)/shard_map/all_to_all | solution.py:12
  165.6 8.1 %all-to-all-done.1 = f32[16,1,2048]{2,1,0:T(1,128)S(1)} async-done(((f32[16,1,2048]{2,1,0:T(1,128)}), f32[16,1,2048]{2,1,0:T(1,128)S(1)}, u32[]{:S(2)}, u32[]{:S(2)}) %all-to-all-start.1) | async-done | bytes 131104 | tf_op jit(solution)/shard_map/all_to_all | solution.py:12
  173.8 5.8 %multiply_convert_fusion = bf16[2048,128]{1,0:T(8,128)(2,1)S(1)} fusion(f32[2048,128]{1,0:T(8,128)S(1)} %get-tuple-element.204, bf16[2048,2048]{1,0:T(8,128)(2,1)} %constant_dynamic-update-slice_fusion.1, bf16[2048,128]{1,0:T(8,128)(2,1)} %param.14, f32[128]{0:T(128)S(1)} %dynamic_slice.17, f32[2048]{0:T(1024)S(1)} %add_rsqrt_fusion), kind=kOutput, calls=%fused_computation.64 | convolution fusion | flops 1076363264 | bytes 10494464 | tf_op jit(solution)/shard_map/dot_general | solution.py:137
  179.6 19.9 %all_to_all.30 = bf16[16,128,128]{2,1,0:T(8,128)(2,1)S(1)} all-to-all(bf16[16,128,128]{2,1,0:T(8,128)(2,1)S(1)} %bitcast.170), channel_id=1, replica_groups=mesh['seq'=8,'mp'=16,'dp'=4] {'mp'}, dimensions={0} | all-to-all | bytes 1048576 | tf_op jit(solution)/shard_map/all_to_all | solution.py:166
  (137 shorter events, 52.3 us)
Async XLA Ops:
  0.0 81.1 %copy-start = (bf16[2048,128]{1,0:T(8,128)(2,1)S(1)}, bf16[2048,128]{1,0:T(8,128)(2,1)}, u32[]{:S(2)}) copy-start(bf16[2048,128]{1,0:T(8,128)(2,1)} %param.12) | copy-start | bytes 1572868
  0.0 33.5 %copy-start.1 = (bf16[2048,128]{1,0:T(8,128)(2,1)S(1)}, bf16[2048,128]{1,0:T(8,128)(2,1)}, u32[]{:S(2)}) copy-start(bf16[2048,128]{1,0:T(8,128)(2,1)} %param.10) | copy-start | bytes 1572868
  0.0 9.6 %collective-permute-start = (bf16[2048,128]{1,0:T(8,128)(2,1)}, bf16[2048,128]{1,0:T(8,128)(2,1)S(1)}, u32[]{:S(2)}, u32[]{:S(2)}) collective-permute-start(bf16[2048,128]{1,0:T(8,128)(2,1)} %param.10), channel_id=1, source_target_pairs={{0,4},{4,8},{8,12},{12,16},{16,20},{20,24},{24,28},{28,32},{32,36}... | collective-permute-start | bytes 1572872 | tf_op jit(solution)/shard_map/ppermute | solution.py:127
  2.7 9.3 %collective-permute-start.1 = (bf16[2048,128]{1,0:T(8,128)(2,1)}, bf16[2048,128]{1,0:T(8,128)(2,1)S(1)}, u32[]{:S(2)}, u32[]{:S(2)}) collective-permute-start(bf16[2048,128]{1,0:T(8,128)(2,1)} %param.10), channel_id=1, source_target_pairs={{0,60},{4,0},{8,4},{12,8},{16,12},{20,16},{24,20},{28,24},{32,28},... | collective-permute-start | bytes 1572872 | tf_op jit(solution)/shard_map/ppermute | solution.py:130
  9.6 7.3 %copy-start.3 = (bf16[2048,128]{1,0:T(8,128)(2,1)}, bf16[2048,128]{1,0:T(8,128)(2,1)S(1)}, u32[]{:S(2)}) copy-start(bf16[2048,128]{1,0:T(8,128)(2,1)S(1)} %collective-permute-done) | copy-start | bytes 1572868
  9.7 8.6 %collective-permute-start.2 = (bf16[2048,128]{1,0:T(8,128)(2,1)S(1)}, bf16[2048,128]{1,0:T(8,128)(2,1)S(1)}, u32[]{:S(2)}, u32[]{:S(2)}) collective-permute-start(bf16[2048,128]{1,0:T(8,128)(2,1)S(1)} %collective-permute-done), channel_id=1, source_target_pairs={{0,4},{4,8},{8,12},{12,16},{16,20},{20,24},{24,28},{28,32},{32,36}... | collective-permute-start | bytes 1572872 | tf_op jit(solution)/shard_map/ppermute | solution.py:127
  12.0 9.4 %copy-start.2 = (bf16[2048,128]{1,0:T(8,128)(2,1)}, bf16[2048,128]{1,0:T(8,128)(2,1)S(1)}, u32[]{:S(2)}) copy-start(bf16[2048,128]{1,0:T(8,128)(2,1)S(1)} %collective-permute-done.1) | copy-start | bytes 1572868
  12.0 9.3 %collective-permute-start.3 = (bf16[2048,128]{1,0:T(8,128)(2,1)S(1)}, bf16[2048,128]{1,0:T(8,128)(2,1)S(1)}, u32[]{:S(2)}, u32[]{:S(2)}) collective-permute-start(bf16[2048,128]{1,0:T(8,128)(2,1)S(1)} %collective-permute-done.1), channel_id=1, source_target_pairs={{0,60},{4,0},{8,4},{12,8},{16,12},{20,16},{24,20},{28,24},{32,28},... | collective-permute-start | bytes 1572872 | tf_op jit(solution)/shard_map/ppermute | solution.py:130
  18.3 9.9 %collective-permute-start.4 = (bf16[2048,128]{1,0:T(8,128)(2,1)S(1)}, bf16[2048,128]{1,0:T(8,128)(2,1)S(1)}, u32[]{:S(2)}, u32[]{:S(2)}) collective-permute-start(bf16[2048,128]{1,0:T(8,128)(2,1)S(1)} %collective-permute-done.2), channel_id=1, source_target_pairs={{0,4},{4,8},{8,12},{12,16},{16,20},{20,24},{24,28},{28,32},{32,36}... | collective-permute-start | bytes 1572872 | tf_op jit(solution)/shard_map/ppermute | solution.py:127
  21.4 15.0 %collective-permute-start.5 = (bf16[2048,128]{1,0:T(8,128)(2,1)S(1)}, bf16[2048,128]{1,0:T(8,128)(2,1)}, u32[]{:S(2)}, u32[]{:S(2)}) collective-permute-start(bf16[2048,128]{1,0:T(8,128)(2,1)S(1)} %collective-permute-done.3), channel_id=1, source_target_pairs={{0,60},{4,0},{8,4},{12,8},{16,12},{20,16},{24,20},{28,24},{32,28},... | collective-permute-start | bytes 1572872 | tf_op jit(solution)/shard_map/ppermute | solution.py:130
  28.2 17.4 %collective-permute-start.6 = (bf16[2048,128]{1,0:T(8,128)(2,1)S(1)}, bf16[2048,128]{1,0:T(8,128)(2,1)}, u32[]{:S(2)}, u32[]{:S(2)}) collective-permute-start(bf16[2048,128]{1,0:T(8,128)(2,1)S(1)} %collective-permute-done.4), channel_id=1, source_target_pairs={{0,4},{4,8},{8,12},{12,16},{16,20},{20,24},{24,28},{28,32},{32,36}... | collective-permute-start | bytes 1572872 | tf_op jit(solution)/shard_map/ppermute | solution.py:127
  36.4 11.1 %collective-permute-start.7 = (bf16[2048,128]{1,0:T(8,128)(2,1)}, bf16[2048,128]{1,0:T(8,128)(2,1)S(1)}, u32[]{:S(2)}, u32[]{:S(2)}) collective-permute-start(bf16[2048,128]{1,0:T(8,128)(2,1)} %collective-permute-done.5), channel_id=1, source_target_pairs={{0,60},{4,0},{8,4},{12,8},{16,12},{20,16},{24,20},{28,24},{32,28},... | collective-permute-start | bytes 1572872 | tf_op jit(solution)/shard_map/ppermute | solution.py:130
  45.6 8.9 %collective-permute-start.8 = (bf16[2048,128]{1,0:T(8,128)(2,1)}, bf16[2048,128]{1,0:T(8,128)(2,1)S(1)}, u32[]{:S(2)}, u32[]{:S(2)}) collective-permute-start(bf16[2048,128]{1,0:T(8,128)(2,1)} %collective-permute-done.6), channel_id=1, source_target_pairs={{0,4},{4,8},{8,12},{12,16},{16,20},{20,24},{24,28},{28,32},{32,36}... | collective-permute-start | bytes 1572872 | tf_op jit(solution)/shard_map/ppermute | solution.py:127
  47.4 11.0 %collective-permute-start.9 = (bf16[2048,128]{1,0:T(8,128)(2,1)S(1)}, bf16[2048,128]{1,0:T(8,128)(2,1)S(1)}, u32[]{:S(2)}, u32[]{:S(2)}) collective-permute-start(bf16[2048,128]{1,0:T(8,128)(2,1)S(1)} %collective-permute-done.7), channel_id=1, source_target_pairs={{0,60},{4,0},{8,4},{12,8},{16,12},{20,16},{24,20},{28,24},{32,28},... | collective-permute-start | bytes 1572872 | tf_op jit(solution)/shard_map/ppermute | solution.py:130
  54.5 9.8 %collective-permute-start.10 = (bf16[2048,128]{1,0:T(8,128)(2,1)S(1)}, bf16[2048,128]{1,0:T(8,128)(2,1)S(1)}, u32[]{:S(2)}, u32[]{:S(2)}) collective-permute-start(bf16[2048,128]{1,0:T(8,128)(2,1)S(1)} %collective-permute-done.8), channel_id=1, source_target_pairs={{0,4},{4,8},{8,12},{12,16},{16,20},{20,24},{24,28},{28,32},{32,36}... | collective-permute-start | bytes 1572872 | tf_op jit(solution)/shard_map/ppermute | solution.py:127
  58.4 8.9 %collective-permute-start.11 = (bf16[2048,128]{1,0:T(8,128)(2,1)S(1)}, bf16[2048,128]{1,0:T(8,128)(2,1)S(1)}, u32[]{:S(2)}, u32[]{:S(2)}) collective-permute-start(bf16[2048,128]{1,0:T(8,128)(2,1)S(1)} %collective-permute-done.9), channel_id=1, source_target_pairs={{0,60},{4,0},{8,4},{12,8},{16,12},{20,16},{24,20},{28,24},{32,28},... | collective-permute-start | bytes 1572872 | tf_op jit(solution)/shard_map/ppermute | solution.py:130
  64.3 9.8 %collective-permute-start.12 = (bf16[2048,128]{1,0:T(8,128)(2,1)S(1)}, bf16[2048,128]{1,0:T(8,128)(2,1)S(1)}, u32[]{:S(2)}, u32[]{:S(2)}) collective-permute-start(bf16[2048,128]{1,0:T(8,128)(2,1)S(1)} %collective-permute-done.10), channel_id=1, source_target_pairs={{0,4},{4,8},{8,12},{12,16},{16,20},{20,24},{24,28},{28,32},{32,36}... | collective-permute-start | bytes 1572872 | tf_op jit(solution)/shard_map/ppermute | solution.py:127
  67.3 8.9 %collective-permute-start.13 = (bf16[2048,128]{1,0:T(8,128)(2,1)S(1)}, bf16[2048,128]{1,0:T(8,128)(2,1)S(1)}, u32[]{:S(2)}, u32[]{:S(2)}) collective-permute-start(bf16[2048,128]{1,0:T(8,128)(2,1)S(1)} %collective-permute-done.11), channel_id=1, source_target_pairs={{0,60},{4,0},{8,4},{12,8},{16,12},{20,16},{24,20},{28,24},{32,28},... | collective-permute-start | bytes 1572872 | tf_op jit(solution)/shard_map/ppermute | solution.py:130
  74.0 6.1 %collective-permute-start.14 = (bf16[2048,128]{1,0:T(8,128)(2,1)S(1)}, bf16[2048,128]{1,0:T(8,128)(2,1)S(1)}, u32[]{:S(2)}, u32[]{:S(2)}) collective-permute-start(bf16[2048,128]{1,0:T(8,128)(2,1)S(1)} %collective-permute-done.12), channel_id=1, source_target_pairs={{0,4},{4,8},{8,12},{12,16},{16,20},{20,24},{24,28},{28,32},{32,36}... | collective-permute-start | bytes 1572872 | tf_op jit(solution)/shard_map/ppermute | solution.py:127
  74.9 11.9 %copy-start.4 = (bf16[2048,128]{1,0:T(8,128)(2,1)S(1)}, bf16[2048,128]{1,0:T(8,128)(2,1)}, u32[]{:S(2)}) copy-start(bf16[2048,128]{1,0:T(8,128)(2,1)} %param.13) | copy-start | bytes 1572868
  86.8 6.6 %copy-start.5 = (bf16[2048,128]{1,0:T(8,128)(2,1)S(1)}, bf16[2048,128]{1,0:T(8,128)(2,1)}, u32[]{:S(2)}) copy-start(bf16[2048,128]{1,0:T(8,128)(2,1)} %param.11) | copy-start | bytes 1572868
  130.1 14.2 %all-to-all-start = ((bf16[8,129,128]{2,1,0:T(8,128)(2,1)}), bf16[8,129,128]{2,1,0:T(8,128)(2,1)S(1)}, u32[]{:S(2)}, u32[]{:S(2)}) async-start(bf16[8,129,128]{2,1,0:T(8,128)(2,1)} %broadcast_in_dim.49), calls=%async_computation | async-start | bytes 557056 | tf_op jit(solution)/shard_map/all_to_all | solution.py:12
  148.5 25.2 %all-to-all-start.1 = ((f32[16,1,2048]{2,1,0:T(1,128)}), f32[16,1,2048]{2,1,0:T(1,128)S(1)}, u32[]{:S(2)}, u32[]{:S(2)}) async-start(f32[16,1,2048]{2,1,0:T(1,128)} %broadcast_in_dim.53), calls=%async_computation.1 | async-start | bytes 262144 | tf_op jit(solution)/shard_map/all_to_all | solution.py:12
